TPU v7x, 32 devices: a whole 2x2x4 slice. The times are simulated.
32 devices in a mesh: expert: 8 (over y, x, core), row: 4 (over z).
Axes of the slice: x: 2, y: 2, z: 4, core: 2. Of those that a mesh axis runs over, the one named last changes fastest.
Arguments:
- weights: bfloat16 [8, 7168, 2048], P('expert', 'row'), may hold values from -6 to 6
- left_bits: int32 [8, 7168], P('expert', 'row'), may hold values from 0 to 1
- right_bits: int32 [8, 2048], P('expert'), may hold values from 0 to 1
- groups: int32 [8, 2048], P('expert'), may hold values from 0 to 15, never falling along the last dimension, each value on 1 to 256 neighbouring positions
Outputs:
- scaled: bfloat16 [8, 7168, 2048], P('expert', 'row')
- block_error: float32 [8, 7168, 256], P('expert', 'row')
- scales: float32 [8, 16], P('expert')
- expert_error: float32 [8], P('expert')
- total_error: float32 [], replicated
Inputs may be any that keep to these rules, and one draw needn't show every extreme that they name: Along each expert's 2048 columns the group number never falls; each of the 16 groups holds 1 to 256 columns.
All inputs are finite; a program needn't handle non-finite values.
Results may differ from a plain program's by a relative error of at most 0.0091.
Values may be sent and summed in bfloat16 or wider, within the bound.
No kernel may reach another device: no remote copies, remote signals or barrier semaphores. Data moves between devices by JAX's collectives and lax.ppermute only.
A program may use at most 192 MiB of HBM per device.

v0:
```python
import math
import jax
import jax.numpy as jnp
from jax import lax
from jax.sharding import PartitionSpec as P

D = 7168
FF = 2048
HB = 128
OUTER = 16
GROUPS = 16
BLOCKS = 56


def sylvester(order):
    row_index = jnp.arange(order, dtype=jnp.int32)[:, None]
    col_index = jnp.arange(order, dtype=jnp.int32)[None, :]
    common = jnp.bitwise_and(row_index, col_index)
    parity = jnp.zeros((order, order), jnp.int32)
    for bit_pos in range(order.bit_length() - 1):
        parity = parity + jnp.bitwise_and(jnp.right_shift(common, bit_pos), 1)
    return (1 - 2 * jnp.bitwise_and(parity, 1)).astype(jnp.float32)


def cosine_block(order):
    first = jnp.arange(order, dtype=jnp.float32)[:, None]
    second = jnp.arange(order, dtype=jnp.float32)[None, :]
    table = math.sqrt(2.0 / order) * jnp.cos(math.pi * (2.0 * second + 1.0) * first / (2.0 * order))
    return jnp.where(first == 0.0, table * math.sqrt(0.5), table)


def coset_error(values):
    nearest = jnp.floor(values + 0.5)
    offset = values - nearest
    squares = jnp.sum(offset * offset, axis=-1)
    largest = jnp.max(jnp.abs(offset), axis=-1)
    parity = jnp.mod(jnp.sum(nearest, axis=-1), 2.0)
    return jnp.where(parity > 0.5, squares + 1.0 - 2.0 * largest, squares)


def lattice_error(values):
    octets = values.reshape(values.shape[:-1] + (values.shape[-1] // 8, 8))
    return jnp.minimum(coset_error(octets), coset_error(octets - 0.5))


def row_transform(mixed_rows, row_hadamard):
    turned = jnp.einsum("eibf,bk->eikf", mixed_rows, row_hadamard, precision=lax.Precision.HIGHEST)
    return turned / math.sqrt(HB)


def weight_of_rows(first_row, count):
    positions = (first_row + jnp.arange(count, dtype=jnp.int32)).astype(jnp.float32)
    return (1.0 + 4.0 * (positions + 0.5) / D) / 3.0


def group_scale(rotated, group_cols):
    column_peak = jnp.max(jnp.abs(rotated), axis=1)
    group_ids = jnp.arange(GROUPS, dtype=jnp.int32)
    in_group = group_cols[:, None, :] == group_ids[None, :, None]
    partial_peak = jnp.max(jnp.where(in_group, column_peak[:, None, :], 0.0), axis=2)
    group_peak = jnp.maximum(lax.pmax(partial_peak, "row"), 1.0)
    column_scale = jnp.sum(jnp.where(in_group, (2.0 / group_peak)[:, :, None], 0.0), axis=1)
    return (group_peak, column_scale)


def body(weights, left_bits, right_bits, groups):
    experts, local_rows, width = weights.shape
    blocks_here = local_rows // HB
    column_hadamard = sylvester(width // OUTER).astype(jnp.bfloat16)
    outer_hadamard = sylvester(OUTER)
    row_hadamard = sylvester(HB)
    block_matrix = cosine_block(BLOCKS).astype(jnp.bfloat16)
    left_sign = (2 * left_bits - 1).astype(jnp.float32)
    right_sign = (2 * right_bits - 1).astype(jnp.float32)
    signed = (weights.astype(jnp.float32) * left_sign[:, :, None] * right_sign[:, None, :]).astype(
        jnp.bfloat16
    )
    shaped = signed.reshape(experts, local_rows, OUTER, width // OUTER)
    inner = jnp.einsum("erpq,qs->erps", shaped, column_hadamard, preferred_element_type=jnp.float32)
    outer = jnp.einsum("erps,pt->erts", inner, outer_hadamard, precision=lax.Precision.HIGHEST)
    columns = (outer.reshape(experts, local_rows, width) / math.sqrt(FF)).astype(jnp.bfloat16)
    blocked = columns.reshape(experts, blocks_here, HB, width)
    own_start = lax.axis_index("row") * blocks_here
    own_matrix = lax.dynamic_slice_in_dim(block_matrix, own_start, blocks_here, 0)
    mixed_rows = jnp.einsum(
        "ij,ejbf->eibf",
        own_matrix,
        lax.all_gather(blocked, "row", axis=1, tiled=True),
        preferred_element_type=jnp.float32,
    )
    rotated = row_transform(mixed_rows, row_hadamard)
    rotated = rotated.reshape(experts, local_rows, width)
    group_peak, column_scale = group_scale(rotated, groups)
    values = rotated * column_scale[:, None, :]
    block_errors = lattice_error(values)
    row_weight = weight_of_rows(lax.axis_index("row") * local_rows, local_rows)
    partial_error = jnp.sum(block_errors * row_weight[None, :, None], axis=(1, 2)) / (D * FF // 8)
    scaled = values.astype(jnp.bfloat16)
    expert_count = experts * lax.axis_size("expert")
    expert_error = lax.psum(partial_error, "row")
    total_error = lax.psum(jnp.sum(expert_error), "expert") / expert_count
    return (scaled, block_errors, group_peak / 2.0, expert_error, total_error)


def solution(mesh):
    placed = (P("expert", "row", None), P("expert", "row"), P("expert", None), P("expert", None))
    return jax.shard_map(
        body,
        mesh=mesh,
        in_specs=placed,
        out_specs=(
            P("expert", "row", None),
            P("expert", "row", None),
            P("expert", None),
            P("expert"),
            P(),
        ),
        check_vma=False,
    )
```

profile of v0, /device:TPU:0, one launch (start us, length us, event | category | flops | bytes accessed | tf_op | source)
XLA Modules:
  0.0 734.2 jit_solution(6547402217888224501)
XLA Ops:
  7.2 0.7 add_convert_fusion
  7.9 0.7 convert_reduce_fusion
  8.6 5.1 fusion.8
  13.7 5.8 copy.28
  19.5 4.3 fusion.25
  23.9 15.7 %fusion.14 = bf16[1,1792,16,128]{3,2,1,0:T(8,128)(2,1)} fusion(f32[1792,16,128]{2,1,0:T(8,128)S(1)} %fusion.25), kind=kOutput, calls=%fused_computation.22 | convolution fusion | flops 711987200 | bytes 22020096 | tf_op jit(solution)/shard_map/erps,pt->erts/dot_general | solution.py:80
  39.6 11.8 %convert_element_type.76 = bf16[1,14,128,2048]{3,2,1,0:T(8,128)(2,1)} reshape(bf16[1,1792,16,128]{3,2,1,0:T(8,128)(2,1)} %fusion.14) | data formatting | bytes 14680064 | tf_op jit(solution)/shard_map/convert_element_type | solution.py:81
  51.4 0.1 dynamic-slice
  51.5 495.9 %all-gather.2.cloned.1.call-done = bf16[1,56,128,2048]{3,2,0,1:T(8,128)(2,1)} async-done(((bf16[1,14,128,2048]{3,2,0,1:T(8,128)(2,1)}), bf16[1,56,128,2048]{3,2,0,1:T(8,128)(2,1)}) %all-gather.2.cloned.1.call-update) | async-done | bytes 29360144 | tf_op jit(solution)/shard_map/all_gather | solution.py:88
  547.4 31.9 %fusion.9 = f32[14,128,2048]{2,0,1:T(8,128)} fusion(bf16[1,56,128,2048]{3,2,0,1:T(8,128)(2,1)} %all-gather.2.cloned.1.call-done, s32[]{:T(128)S(6)} %select_n.94, f32[56]{0:T(128)S(1)} %add_multiply_fusion.2, pred[14]{0:T(512)(128)(4,1)S(1)} %dynamic-slice), kind=kOutput, calls=%fused_computation.21 | convolution fusion | flops 411048064 | bytes 44040432 | tf_op jit(solution)/shard_map/ij,ejbf->eibf/dot_general | solution.py:85
  579.3 29.6 %abs_reduce_fusion.2 = (f32[2048]{0:T(1024)S(1)}, f32[128,14,2048]{2,0,1:T(8,128)}) fusion(f32[14,128,2048]{2,0,1:T(8,128)} %fusion.9), kind=kOutput, calls=%fused_computation.15 | convolution fusion | flops 5648562176 | bytes 29368320 | tf_op jit(solution)/shard_map/eibf,bk->eikf/dot_general | solution.py:47
  608.9 0.1 select_reduce_fusion.1
  609.0 8.9 %pmax.7 = f32[1,16]{1,0:T(1,128)S(1)} all-reduce(f32[1,16]{1,0:T(1,128)S(1)} %bitcast.114), channel_id=1, replica_groups=mesh['expert'=8,'row'=4] {'row'}, use_global_device_ids=true, to_apply=%region_2.3 | all-reduce | flops 16 | bytes 128 | tf_op jit(solution)/shard_map/pmax | solution.py:61
  617.9 0.5 maximum_multiply_fusion
  618.4 0.1 select_reduce_fusion
  618.5 0.1 mul.276
  618.6 10.4 %fusion.3 = bf16[1,1792,2048]{2,1,0:T(8,128)(2,1)} fusion(f32[128,14,2048]{2,0,1:T(8,128)} %get-tuple-element.26, f32[2048]{0:T(1024)S(1)} %select_reduce_fusion), kind=kLoop, calls=%fused_computation.4 | loop fusion | flops 7340032 | bytes 22028288 | tf_op jit(solution)/shard_map/convert_element_type | solution.py:98
  629.0 17.6 %copy.24 = f32[1,14,128,2048]{2,1,3,0:T(8,128)} copy(f32[1,14,128,2048]{3,2,1,0:T(8,128)} %bitcast.108) | data formatting | bytes 29360128 | tf_op jit(solution)/shard_map/div | solution.py:48
  646.6 16.9 %reshape.599 = f32[1,1792,256,8]{1,3,2,0:T(8,128)} reshape(f32[1,14,128,2048]{2,1,3,0:T(8,128)} %copy.24) | data formatting | bytes 29360128 | tf_op jit(solution)/shard_map/reshape | solution.py:92
  663.5 32.5 %fusion.7 = (f32[1792,256]{0,1:T(8,128)S(1)}, f32[1792,256]{0,1:T(8,128)S(1)}, f32[1792,256]{0,1:T(8,128)S(1)}, f32[1792,256]{0,1:T(8,128)S(1)}, f32[1792,256]{0,1:T(8,128)S(1)}, /*index=5*/f32[1792,256]{0,1:T(8,128)S(1)}) fusion(f32[1,1792,256,8]{1,3,2,0:T(8,128)} %reshape.599, f32[256,8]{1,0:T(8,128)S(1)} %mul.276), kind=kLoop, calls=%fused_computation.14 | loop fusion | flops 59637760 | bytes 25698304 | tf_op jit(solution)/shard_map/reduce_sum | solution.py:37
  696.0 3.2 multiply_reduce_fusion.2
  699.3 1.7 copy.25
  701.6 11.3 %psum.14 = f32[1]{0:T(128)} all-reduce(f32[1]{0:T(128)} %bitcast.25), channel_id=1, replica_groups=mesh['expert'=8,'row'=4] {'row'}, use_global_device_ids=true, to_apply=%region_11.12 | all-reduce | flops 1 | bytes 8 | tf_op jit(solution)/shard_map/psum | solution.py:100
  712.9 12.4 %psum.15 = f32[]{:T(128)} all-reduce(f32[]{:T(128)} %bitcast.26), channel_id=1, replica_groups=mesh['expert'=8,'row'=4] {'expert'}, use_global_device_ids=true, to_apply=%region_12.13 | all-reduce | flops 1 | bytes 8 | tf_op jit(solution)/shard_map/psum | solution.py:101
  (7 shorter events, 0.1 us)
Async XLA Ops:
  7.2 540.2 %all-gather.2.cloned.1.call-start = ((), (), s32[]{:S(2)}) async-start(), calls=%async_computation | async-start | bytes 36700160 | tf_op jit(solution)/shard_map/all_gather | solution.py:88
  579.3 29.6 %copy-start = (s32[1,2048]{1,0:T(1,128)S(1)}, s32[1,2048]{1,0:T(1,128)}, u32[]{:S(2)}) copy-start(s32[1,2048]{1,0:T(1,128)} %param.7) | copy-start | bytes 24580
Sparse Core Ops, SparseCore 0:
  51.5 495.8 all-gather.1
where the time goes:
time: 743 us; the launch traced here: 734 us
  waiting for transfers between devices  496 us (67%)
  matrix products  81.6 us (11%)
  local copies, waits for them, and re-layouts  53.9 us (7%)
  other arithmetic  53.5 us (7%)
  blocking collectives  32.6 us (4%)
  between operations  16.7 us (2%)
    all_gather x1, waiting for transfers between devices, body(): lax.all_gather(blocked, 'row', axis=1, tiled=True)  496 us
    reduce_sum x1, other arithmetic, coset_error(): parity = jnp.mod(jnp.sum(nearest, axis=-1), 2.0)  32.5 us
    dot_general x1, matrix products, body(): jnp.einsum('ij,ejbf->eibf', own_matrix, lax.all_gather(blocked, 'row', ax...  31.9 us
    dot_general x1, matrix products, row_transform(): jnp.einsum('eibf,bk->eikf', mixed_rows, row_hadamard, precision=lax.Preci...  29.6 us
    div x1, local copies, waits for them, and re-layouts, row_transform(): return turned / math.sqrt(HB)  17.6 us
    reshape x1, local copies, waits for them, and re-layouts, body(): rotated = rotated.reshape(experts, local_rows, width)  16.9 us
    dot_general x1, matrix products, body(): jnp.einsum('erps,pt->erts', inner, outer_hadamard, precision=lax.Precisio...  15.7 us
  transfers between devices with their start and end apart: 1, of which 1 were waited for; matrix products, arithmetic and copies ran while one was open for 0% of the time, Pallas kernels for 0%

commit v1 on v0

--- a/solution.py
+++ b/solution.py
@@ -82,12 +82,26 @@
     blocked = columns.reshape(experts, blocks_here, HB, width)
     own_start = lax.axis_index("row") * blocks_here
     own_matrix = lax.dynamic_slice_in_dim(block_matrix, own_start, blocks_here, 0)
+    devices, mine = (lax.axis_size("row"), lax.axis_index("row"))
+    left = [(i, (i - 1) % devices) for i in range(devices)]
+    extent = blocked.shape[1]
+    held = blocked
     mixed_rows = jnp.einsum(
         "ij,ejbf->eibf",
-        own_matrix,
-        lax.all_gather(blocked, "row", axis=1, tiled=True),
+        lax.dynamic_slice_in_dim(own_matrix, mine * extent, held.shape[1], axis=1),
+        held,
         preferred_element_type=jnp.float32,
     )
+    for step in range(1, devices):
+        held = lax.ppermute(held, "row", left)
+        mixed_rows = mixed_rows + jnp.einsum(
+            "ij,ejbf->eibf",
+            lax.dynamic_slice_in_dim(
+                own_matrix, (mine + step) % devices * extent, held.shape[1], axis=1
+            ),
+            held,
+            preferred_element_type=jnp.float32,
+        )
     rotated = row_transform(mixed_rows, row_hadamard)
     rotated = rotated.reshape(experts, local_rows, width)
     group_peak, column_scale = group_scale(rotated, groups)

time: 743 us -> 723 us (0.973)
  waiting for transfers between devices: 496 us -> 420 us
  matrix products: 81.6 us -> 119 us
  local copies, waits for them, and re-layouts: 53.9 us -> 69 us
  starting transfers between devices: 0.04 us -> 13.6 us
  between operations: 16.7 us -> 3.39 us
    all_gather x1 -> x0, waiting for transfers between devices: 496 us -> none  [body(): lax.all_gather(blocked, 'row', axis=1, tiled=True)]
    ppermute x0 -> x3, waiting for transfers between devices: none -> 420 us  [body(): held = lax.ppermute(held, 'row', left)]
    dot_general x1 -> x4, matrix products: 31.9 us -> 69.1 us  [the longest x3 55.6 us: body(): jnp.einsum('ij,ejbf->eibf', lax.dynamic_slice_in_dim(own_matrix, (mine +...]
    ppermute x0 -> x3, starting transfers between devices: none -> 13.6 us  [body(): held = lax.ppermute(held, 'row', left)]
    convert_element_type x1 -> x2, local copies, waits for them, and re-layouts: 11.8 us -> 23.9 us  [body(): (outer.reshape(experts, local_rows, width) / math.sqrt(FF)).astype(jnp.bf...]
  transfers between devices with their start and end apart: 1 -> 3, of which waited for: 1 -> 3; matrix products, arithmetic and copies ran while one was open for 0% -> 7% of each run, Pallas kernels for 0% -> 0%
where the time goes in v1:
time: 723 us; the launch traced here: 713 us
  waiting for transfers between devices  420 us (58%)
  matrix products  119 us (16%)
  local copies, waits for them, and re-layouts  69 us (10%)
  other arithmetic  53.6 us (7%)
  blocking collectives  34.8 us (5%)
  starting transfers between devices  13.6 us (2%)
    ppermute x3, waiting for transfers between devices, body(): held = lax.ppermute(held, 'row', left)  420 us
    dot_general x3, matrix products, body(): jnp.einsum('ij,ejbf->eibf', lax.dynamic_slice_in_dim(own_matrix, (mine +...  55.6 us
    reduce_sum x1, other arithmetic, coset_error(): parity = jnp.mod(jnp.sum(nearest, axis=-1), 2.0)  32.5 us
    dot_general x1, matrix products, row_transform(): jnp.einsum('eibf,bk->eikf', mixed_rows, row_hadamard, precision=lax.Preci...  29.8 us
    convert_element_type x2, local copies, waits for them, and re-layouts, body(): (outer.reshape(experts, local_rows, width) / math.sqrt(FF)).astype(jnp.bf...  23.9 us
    div x1, local copies, waits for them, and re-layouts, row_transform(): return turned / math.sqrt(HB)  17.6 us
    reshape x1, local copies, waits for them, and re-layouts, body(): rotated = rotated.reshape(experts, local_rows, width)  16.9 us
    dot_general x1, matrix products, body(): jnp.einsum('erps,pt->erts', inner, outer_hadamard, precision=lax.Precisio...  15.7 us
  transfers between devices with their start and end apart: 3, of which 3 were waited for; matrix products, arithmetic and copies ran while one was open for 7% of the time, Pallas kernels for 0%

profile of v1, /device:TPU:0, one launch (start us, length us, event | category | flops | bytes accessed | tf_op | source)
XLA Modules:
  0.0 713.5 jit_solution(14558997916857791400)
XLA Ops:
  2.1 5.1 fusion.16
  7.1 5.8 copy.34
  12.9 4.4 fusion.32
  17.3 15.7 %fusion.21 = bf16[1,1792,16,128]{3,2,1,0:T(8,128)(2,1)} fusion(f32[1792,16,128]{2,1,0:T(8,128)S(1)} %fusion.32), kind=kOutput, calls=%fused_computation.30 | convolution fusion | flops 711987200 | bytes 22020096 | tf_op jit(solution)/shard_map/erps,pt->erts/dot_general | solution.py:80
  33.0 11.8 %convert_element_type.90 = bf16[1,14,128,2048]{3,2,1,0:T(8,128)(2,1)} reshape(bf16[1,1792,16,128]{3,2,1,0:T(8,128)(2,1)} %fusion.21) | data formatting | bytes 14680064 | tf_op jit(solution)/shard_map/convert_element_type | solution.py:81
  44.8 5.1 collective-permute-start
  49.9 157.6 %collective-permute-done = bf16[1,14,128,2048]{3,2,1,0:T(8,128)(2,1)S(1)} collective-permute-done((bf16[1,14,128,2048]{3,2,1,0:T(8,128)(2,1)}, bf16[1,14,128,2048]{3,2,1,0:T(8,128)(2,1)S(1)}, u32[]{:S(2)}, u32[]{:S(2)}) %collective-permute-start) | collective-permute-done | bytes 7340064 | tf_op jit(solution)/shard_map/ppermute | solution.py:96
  210.4 4.2 collective-permute-start.1
  214.6 156.4 %collective-permute-done.1 = bf16[1,14,128,2048]{3,2,1,0:T(8,128)(2,1)} collective-permute-done((bf16[1,14,128,2048]{3,2,1,0:T(8,128)(2,1)S(1)}, bf16[1,14,128,2048]{3,2,1,0:T(8,128)(2,1)}, u32[]{:S(2)}, u32[]{:S(2)}) %collective-permute-start.1) | collective-permute-done | bytes 7340064 | tf_op jit(solution)/shard_map/ppermute | solution.py:96
  371.0 4.4 collective-permute-start.2
  375.4 12.1 %convert_element_type.88 = bf16[14,128,2048]{2,1,0:T(8,128)(2,1)} reshape(bf16[1,1792,16,128]{3,2,1,0:T(8,128)(2,1)} %fusion.21) | data formatting | bytes 14680064 | tf_op jit(solution)/shard_map/convert_element_type | solution.py:81
  387.7 13.5 %fusion.14 = f32[128,2048,14]{1,2,0:T(8,128)} fusion(bf16[14,128,2048]{2,1,0:T(8,128)(2,1)} %convert_element_type.88, bf16[56,56]{1,0:T(8,128)(2,1)S(1)} %select_convert_fusion, s32[]{:T(128)S(6)} %select_n.134), kind=kOutput, calls=%fused_computation.26 | convolution fusion | flops 102760448 | bytes 22024196 | tf_op jit(solution)/shard_map/ij,ejbf->eibf/dot_general | solution.py:89
  401.2 10.3 %fusion.9 = f32[128,2048,14]{1,2,0:T(8,128)} fusion(bf16[1,14,128,2048]{3,2,1,0:T(8,128)(2,1)S(1)} %bitcast.127, bf16[56,56]{1,0:T(8,128)(2,1)S(1)} %select_convert_fusion, s32[]{:T(128)S(6)} %select_n.134, s32[]{:T(128)S(6)} %select_n.137), kind=kOutput, calls=%fused_computation.21 | convolution fusion | flops 102760448 | bytes 22024200 | tf_op jit(solution)/shard_map/ij,ejbf->eibf/dot_general | solution.py:97
  411.5 13.5 %fusion.7 = f32[128,2048,14]{1,2,0:T(8,128)} fusion(bf16[1,14,128,2048]{3,2,1,0:T(8,128)(2,1)} %collective-permute-done.1, bf16[56,56]{1,0:T(8,128)(2,1)S(1)} %select_convert_fusion, s32[]{:T(128)S(6)} %select_n.134, s32[]{:T(128)S(6)} %select_n.140), kind=kOutput, calls=%fused_computation.19 | convolution fusion | flops 102760448 | bytes 22024200 | tf_op jit(solution)/shard_map/ij,ejbf->eibf/dot_general | solution.py:97
  425.0 106.2 %collective-permute-done.2 = bf16[1,14,128,2048]{3,2,1,0:T(8,128)(2,1)} collective-permute-done((bf16[1,14,128,2048]{3,2,1,0:T(8,128)(2,1)}, bf16[1,14,128,2048]{3,2,1,0:T(8,128)(2,1)}, u32[]{:S(2)}, u32[]{:S(2)}) %collective-permute-start.2) | collective-permute-done | bytes 7340064 | tf_op jit(solution)/shard_map/ppermute | solution.py:96
  531.2 31.9 %add_bitcast_fusion = f32[14,128,2048]{2,0,1:T(8,128)} fusion(f32[128,2048,14]{1,2,0:T(8,128)} %fusion.7, f32[128,2048,14]{1,2,0:T(8,128)} %fusion.14, f32[128,2048,14]{1,2,0:T(8,128)} %fusion.9, bf16[1,14,128,2048]{3,2,1,0:T(8,128)(2,1)} %collective-permute-done.2, bf16[56,56]{1,0:T(8,128)(2,1)S(1)} %select_convert_fusion, s32[]{:T(128)S(6)} %select_n.134, ...), kind=kOutput, calls=%fused_computation | convolution fusion | flops 113770496 | bytes 66064392 | tf_op jit(solution)/shard_map/ij,ejbf->eibf/dot_general | solution.py:97
  563.1 29.8 %abs_reduce_fusion.2 = (f32[2048]{0:T(1024)S(1)}, f32[128,14,2048]{2,0,1:T(8,128)}) fusion(f32[14,128,2048]{2,0,1:T(8,128)} %add_bitcast_fusion), kind=kOutput, calls=%fused_computation.13 | convolution fusion | flops 5648562176 | bytes 29368320 | tf_op jit(solution)/shard_map/eibf,bk->eikf/dot_general | solution.py:47
  593.0 12.8 %pmax.7 = f32[1,16]{1,0:T(1,128)S(1)} all-reduce(f32[1,16]{1,0:T(1,128)S(1)} %bitcast.131), channel_id=1, replica_groups=mesh['expert'=8,'row'=4] {'row'}, use_global_device_ids=true, to_apply=%region_2.3 | all-reduce | flops 16 | bytes 128 | tf_op jit(solution)/shard_map/pmax | solution.py:61
  606.6 10.4 %fusion = bf16[1,1792,2048]{2,1,0:T(8,128)(2,1)} fusion(f32[128,14,2048]{2,0,1:T(8,128)} %get-tuple-element.26, f32[2048]{0:T(1024)S(1)} %select_reduce_fusion), kind=kLoop, calls=%fused_computation.2 | loop fusion | flops 7340032 | bytes 22028288 | tf_op jit(solution)/shard_map/convert_element_type | solution.py:112
  617.0 17.6 %copy.30 = f32[1,14,128,2048]{2,1,3,0:T(8,128)} copy(f32[1,14,128,2048]{3,2,1,0:T(8,128)} %bitcast.124) | data formatting | bytes 29360128 | tf_op jit(solution)/shard_map/div | solution.py:48
  634.6 16.9 %reshape.621 = f32[1,1792,256,8]{1,3,2,0:T(8,128)} reshape(f32[1,14,128,2048]{2,1,3,0:T(8,128)} %copy.30) | data formatting | bytes 29360128 | tf_op jit(solution)/shard_map/reshape | solution.py:106
  651.5 32.5 %fusion.4 = (f32[1792,256]{0,1:T(8,128)S(1)}, f32[1792,256]{0,1:T(8,128)S(1)}, f32[1792,256]{0,1:T(8,128)S(1)}, f32[1792,256]{0,1:T(8,128)S(1)}, f32[1792,256]{0,1:T(8,128)S(1)}, /*index=5*/f32[1792,256]{0,1:T(8,128)S(1)}) fusion(f32[1,1792,256,8]{1,3,2,0:T(8,128)} %reshape.621, f32[256,8]{1,0:T(8,128)S(1)} %mul.331), kind=kLoop, calls=%fused_computation.12 | loop fusion | flops 59637760 | bytes 25698304 | tf_op jit(solution)/shard_map/reduce_sum | solution.py:37
  689.6 9.5 %psum.14 = f32[1]{0:T(128)} all-reduce(f32[1]{0:T(128)} %bitcast.30), channel_id=1, replica_groups=mesh['expert'=8,'row'=4] {'row'}, use_global_device_ids=true, to_apply=%region_11.12 | all-reduce | flops 1 | bytes 8 | tf_op jit(solution)/shard_map/psum | solution.py:114
  699.1 12.4 %psum.15 = f32[]{:T(128)} all-reduce(f32[]{:T(128)} %bitcast.31), channel_id=1, replica_groups=mesh['expert'=8,'row'=4] {'expert'}, use_global_device_ids=true, to_apply=%region_12.13 | all-reduce | flops 1 | bytes 8 | tf_op jit(solution)/shard_map/psum | solution.py:115
  (21 shorter events, 10.3 us)
Async XLA Ops:
  44.8 162.6 %collective-permute-start = (bf16[1,14,128,2048]{3,2,1,0:T(8,128)(2,1)}, bf16[1,14,128,2048]{3,2,1,0:T(8,128)(2,1)S(1)}, u32[]{:S(2)}, u32[]{:S(2)}) collective-permute-start(bf16[1,14,128,2048]{3,2,1,0:T(8,128)(2,1)} %convert_element_type.90), channel_id=1, source_target_pairs={{0,3},{1,0},{2,1},{3,2},{4,7},{5,4},{6,5},{7,6},{8,11},{9,8},{10,9... | collective-permute-start | bytes 22020104 | tf_op jit(solution)/shard_map/ppermute | solution.py:96
  207.4 3.0 copy-start
  210.4 160.6 %collective-permute-start.1 = (bf16[1,14,128,2048]{3,2,1,0:T(8,128)(2,1)S(1)}, bf16[1,14,128,2048]{3,2,1,0:T(8,128)(2,1)}, u32[]{:S(2)}, u32[]{:S(2)}) collective-permute-start(bf16[1,14,128,2048]{3,2,1,0:T(8,128)(2,1)S(1)} %collective-permute-done), channel_id=1, source_target_pairs={{0,3},{1,0},{2,1},{3,2},{4,7},{5,4},{6,5},{7,6},{8,11},{9,8},{10,9... | collective-permute-start | bytes 22020104 | tf_op jit(solution)/shard_map/ppermute | solution.py:96
  371.0 160.2 %collective-permute-start.2 = (bf16[1,14,128,2048]{3,2,1,0:T(8,128)(2,1)}, bf16[1,14,128,2048]{3,2,1,0:T(8,128)(2,1)}, u32[]{:S(2)}, u32[]{:S(2)}) collective-permute-start(bf16[1,14,128,2048]{3,2,1,0:T(8,128)(2,1)} %collective-permute-done.1), channel_id=1, source_target_pairs={{0,3},{1,0},{2,1},{3,2},{4,7},{5,4},{6,5},{7,6},{8,11},{9,8},{10,9... | collective-permute-start | bytes 22020104 | tf_op jit(solution)/shard_map/ppermute | solution.py:96
  375.4 25.8 %slice-start = ((s8[7340032]{0:T(1024)(128)(4,1)}), s8[3145728]{0:T(1024)(128)(4,1)S(1)}, s32[]{:S(2)}) async-start(s8[7340032]{0:T(1024)(128)(4,1)} %bitcast.126), calls=%async_computation | async-start | bytes 6291456
  387.7 13.5 %slice-start.1 = ((s8[7340032]{0:T(1024)(128)(4,1)}), s8[4194304]{0:T(1024)(128)(4,1)S(1)}, s32[]{:S(2)}) async-start(s8[7340032]{0:T(1024)(128)(4,1)} %bitcast.126), calls=%async_computation.1 | async-start | bytes 8388608
  563.1 29.8 %copy-start.1 = (s32[1,2048]{1,0:T(1,128)S(1)}, s32[1,2048]{1,0:T(1,128)}, u32[]{:S(2)}) copy-start(s32[1,2048]{1,0:T(1,128)} %param.7) | copy-start | bytes 24580
